TPU v7x, 32 devices: a whole 2x2x4 slice. The times are simulated.
32 devices in a mesh: tile: 8 (over y, x, core), bulk: 4 (over z).
Axes of the slice: x: 2, y: 2, z: 4, core: 2. Of those that a mesh axis runs over, the one named last changes fastest.
Arguments:
- integrals: bfloat16 [96, 256, 768], P(('tile', 'bulk')), may hold values from -0.21875 to 0.21875
- amplitudes: bfloat16 [4, 768, 1024], P(None, 'bulk', 'tile'), may hold values from -6 to 6
- residual_in: bfloat16 [96, 256, 1024], P(('tile', 'bulk')), may hold values from -6 to 6
- tile_irrep: int32 [96], replicated, may hold values from 0 to 3, as said below
Outputs:
- residual: bfloat16 [96, 256, 1024], P(('tile', 'bulk'))
Inputs may be any that keep to these rules, and one draw needn't show every extreme that they name: tile_irrep never falls along the tiles, and every irrep labels at least 12 tiles.
All inputs are finite; a program needn't handle non-finite values.
Results may differ from a plain program's by a relative error of at most 0.001.
Values may be sent and summed in bfloat16 or wider, within the bound.
A program may use at most 64 MiB of HBM per device.

v0:
```python
import jax
import jax.numpy as jnp
from jax import lax
from jax.sharding import PartitionSpec as P


def local(integrals, amplitudes, residual_in, tile_irrep):
    tile_dev = integrals.shape[0]
    row_index = lax.axis_index("tile")
    col_index = lax.axis_index("bulk")
    bulk_count = lax.axis_size("bulk")
    first_tile = (row_index * bulk_count + col_index) * tile_dev
    local_irrep = lax.dynamic_slice_in_dim(tile_irrep, first_tile, tile_dev, 0)
    whole_cd = lax.all_gather(amplitudes, "bulk", axis=1, tiled=True)
    picked = jnp.take(lax.all_gather(whole_cd, "tile", axis=2, tiled=True), local_irrep, axis=0)
    product = jnp.einsum("trc,tcp->trp", integrals, picked, preferred_element_type=jnp.float32)
    return (residual_in.astype(jnp.float32) + product).astype(jnp.bfloat16)


def solution(mesh):
    return jax.shard_map(
        local,
        mesh=mesh,
        in_specs=(
            P(("tile", "bulk"), None, None),
            P(None, "bulk", "tile"),
            P(("tile", "bulk"), None, None),
            P(),
        ),
        out_specs=P(("tile", "bulk"), None, None),
        check_vma=False,
    )
```

profile of v0, /device:TPU:1, one launch (start us, length us, event | category | flops | bytes accessed | tf_op | source)
XLA Modules:
  0.0 95.6 jit_solution(11539856115014887911)
XLA Ops:
  6.5 0.0 copy-start
  6.5 0.0 copy-start.1
  6.5 0.0 all-gather.2.cloned.1.call-start
  6.5 18.7 %all_gather.6 = bf16[4,768,128]{2,1,0:T(8,128)(2,1)} all-gather(bf16[4,192,128]{2,1,0:T(8,128)(2,1)} %param.5), channel_id=1, replica_groups=mesh['tile'=8,'bulk'=4] {'bulk'}, dimensions={1}, use_global_device_ids=true | all-gather | bytes 983040 | tf_op jit(solution)/shard_map/all_gather | solution.py:14
  25.3 0.0 all-gather.2.cloned.1.call-update
  25.3 1.7 %copy.5 = bf16[3,256,1024]{1,2,0:T(8,128)(2,1)S(1)} copy(bf16[3,256,1024]{2,1,0:T(8,128)(2,1)} %param.6) | data formatting | bytes 3145728 | tf_op args[2]
  27.0 0.0 copy-done.1
  27.1 0.1 compare_and_fusion
  27.1 47.6 %all-gather.2.cloned.1.call-done = bf16[4,768,1024]{2,1,0:T(8,128)(2,1)} async-done(((bf16[4,768,128]{2,1,0:T(8,128)(2,1)}), bf16[4,768,1024]{2,1,0:T(8,128)(2,1)}) %all-gather.2.cloned.1.call-update) | async-done | bytes 6291472 | tf_op jit(solution)/shard_map/all_gather | solution.py:15
  74.8 6.0 %gather_fusion = bf16[3,768,1024]{2,1,0:T(8,128)(2,1)} fusion(bf16[4,768,1024]{2,1,0:T(8,128)(2,1)} %all-gather.2.cloned.1.call-done, s32[1024]{0:T(1024)S(1)} %pad_clamp_fusion), kind=kCustom, calls=%fused_computation | custom fusion | bytes 9437196 | tf_op jit(solution)/shard_map/jit(_take)/gather | solution.py:15
  80.8 0.0 copy-done
  80.8 5.4 %fusion.3 = bf16[3,256,1024]{1,2,0:T(8,128)(2,1)} fusion(bf16[3,256,1024]{1,2,0:T(8,128)(2,1)S(1)} %copy.5, bf16[3,256,768]{2,1,0:T(8,128)(2,1)S(1)} %copy-done, bf16[3,768,1024]{2,1,0:T(8,128)(2,1)} %gather_fusion, pred[3]{0:T(512)(128)(4,1)S(1)} %get-tuple-element.5), kind=kOutput, calls=%fused_computation.5 | convolution fusion | flops 1212678144 | bytes 9043971 | tf_op jit(solution)/shard_map/trc,tcp->trp/dot_general | solution.py:16
  86.2 2.6 %copy.7 = bf16[3,256,1024]{2,1,0:T(8,128)(2,1)} copy(bf16[3,256,1024]{1,2,0:T(8,128)(2,1)} %fusion.3) | data formatting | bytes 3145728 | tf_op jit(solution)/shard_map/convert_element_type | solution.py:17
  (1 shorter events, 0.0 us)
Async XLA Ops:
  6.5 74.2 %copy-start = (bf16[3,256,768]{2,1,0:T(8,128)(2,1)S(1)}, bf16[3,256,768]{2,1,0:T(8,128)(2,1)}, u32[]{:S(2)}) copy-start(bf16[3,256,768]{2,1,0:T(8,128)(2,1)} %param.4) | copy-start | bytes 3538948
  6.5 20.5 %copy-start.1 = (s32[96]{0:T(128)S(1)}, s32[96]{0:T(128)}, u32[]{:S(2)}) copy-start(s32[96]{0:T(128)} %param.7) | copy-start | bytes 1156
  6.5 68.2 %all-gather.2.cloned.1.call-start = ((), (), s32[]{:S(2)}) async-start(), calls=%async_computation | async-start | bytes 7077888 | tf_op jit(solution)/shard_map/all_gather | solution.py:15
Sparse Core Ops, SparseCore 0:
  25.4 49.2 all-gather.1
where the time goes:
time: 96.1 us; the launch traced here: 95.6 us
  waiting for transfers between devices  47.6 us (50%)
  blocking collectives  18.7 us (19%)
  between operations  13.4 us (14%)
  local copies, waits for them, and re-layouts  10.3 us (11%)
  matrix products  5.4 us (6%)
    all_gather x1, waiting for transfers between devices, local(): lax.all_gather(whole_cd, 'tile', axis=2, tiled=True)  47.6 us
    all_gather x1, blocking collectives, local(): whole_cd = lax.all_gather(amplitudes, 'bulk', axis=1, tiled=True)  18.7 us
    gather x1, local copies, waits for them, and re-layouts, local(): jnp.take(lax.all_gather(whole_cd, 'tile', axis=2, tiled=True), local_irre...  6.01 us
    dot_general x1, matrix products, local(): jnp.einsum('trc,tcp->trp', integrals, picked, preferred_element_type=jnp....  5.4 us
    convert_element_type x1, local copies, waits for them, and re-layouts, local(): return (residual_in.astype(jnp.float32) + product).astype(jnp.bfloat16)  2.58 us
  transfers between devices with their start and end apart: 1, of which 1 were waited for; matrix products, arithmetic and copies ran while one was open for 2% of the time, Pallas kernels for 0%

commit v1 on v0

v1 whole, which is shorter than its diff:
```python
import functools

import jax
import jax.numpy as jnp
from jax import lax
from jax.experimental import pallas as pl
from jax.experimental.pallas import tpu as pltpu
from jax.sharding import PartitionSpec as P

MESH = pl.DeviceIdType.MESH
PARTS = 2


def gathered_plan(integrals, amplitudes, residual_in, tile_irrep):
    tile_dev = integrals.shape[0]
    first_tile = (lax.axis_index("tile") * lax.axis_size("bulk") + lax.axis_index("bulk")) * tile_dev
    local_irrep = lax.dynamic_slice_in_dim(tile_irrep, first_tile, tile_dev, 0)
    whole_cd = lax.all_gather(amplitudes, "bulk", axis=1, tiled=True)
    picked = jnp.take(lax.all_gather(whole_cd, "tile", axis=2, tiled=True), local_irrep, axis=0)
    product = jnp.einsum("trc,tcp->trp", integrals, picked, preferred_element_type=jnp.float32)
    return (residual_in.astype(jnp.float32) + product).astype(jnp.bfloat16)


def kernel(rows, bulk, slots, parts, irrep_ref, amp_hbm, int_hbm, res_hbm, out_ref, *scratch):
    cols = rows // 2
    offsets = [0] + [s * d for d in range(1, bulk) for s in (-1, 1)]
    chunks = len(offsets)
    (amp, ints, res, whole), scratch = scratch[:4], scratch[4:]
    held = [[None] * parts] + [list(scratch[i * parts:(i + 1) * parts]) for i in range(chunks - 1)]
    scratch = scratch[(chunks - 1) * parts:]
    picked = [list(scratch[i * parts:(i + 1) * parts]) for i in range(chunks)]
    (z_send, z_recv, c_send, c_recv, p_send, p_recv, local_sem) = scratch[chunks * parts:]
    tiles = ints.shape[0]
    irreps, depth, width = amp.shape
    piece = depth // parts
    me, at = lax.axis_index("tile"), lax.axis_index("bulk")
    col, core = me // 2, me % 2
    partner = col * 2 + (1 - core)

    amp_copy = pltpu.make_async_copy(amp_hbm, amp, local_sem.at[0])
    int_copy = pltpu.make_async_copy(int_hbm, ints, local_sem.at[1])
    res_copy = pltpu.make_async_copy(res_hbm, res, local_sem.at[2])
    amp_copy.start()

    barrier = pltpu.get_barrier_semaphore()
    pl.semaphore_signal(barrier, inc=1, device_id=(partner, at), device_id_type=MESH)
    for j in range(1, cols):
        pl.semaphore_signal(barrier, inc=1, device_id=(lax.rem(col + j, cols) * 2 + core, at), device_id_type=MESH)

    @pl.when(at > 0)
    def _():
        pl.semaphore_signal(barrier, inc=1, device_id=(me, at - 1), device_id_type=MESH)

    @pl.when(at < bulk - 1)
    def _():
        pl.semaphore_signal(barrier, inc=1, device_id=(me, at + 1), device_id_type=MESH)

    int_copy.start()
    res_copy.start()
    pl.semaphore_wait(barrier, cols + (at > 0).astype(jnp.int32) + (at < bulk - 1).astype(jnp.int32))

    amp_copy.wait()

    def block(c, p):
        if c == 0:
            return amp.at[:, pl.ds(p * piece, piece), :]
        return held[c][p]

    def line(c, p, step):
        there = offsets.index(offsets[c] - step)
        way = 0 if step > 0 else 1
        return pltpu.make_async_remote_copy(
            src_ref=block(c, p), dst_ref=held[there][p], send_sem=z_send.at[way, c, p],
            recv_sem=z_recv.at[there, p], device_id=(me, at + step), device_id_type=MESH)

    def line_in(c, p):
        return pltpu.make_async_remote_copy(
            src_ref=held[c][p], dst_ref=held[c][p], send_sem=z_send.at[0, c, p],
            recv_sem=z_recv.at[c, p], device_id=(partner, at), device_id_type=MESH)

    def slab(c, p, row):
        first = pl.multiple_of((at + offsets[c]) * depth + p * piece, 16)
        return whole.at[:, pl.ds(first, piece), pl.ds(pl.multiple_of(row * width, 128), width)]

    def across(c, p, j):
        return pltpu.make_async_remote_copy(
            src_ref=picked[c][p].at[j - 1], dst_ref=slab(c, p, me), send_sem=c_send.at[c, p, j],
            recv_sem=c_recv.at[c, p, j], device_id=(lax.rem(col + j, cols) * 2 + core, at), device_id_type=MESH)

    def over(c, p, j, side):
        row = lax.rem(col - j + cols, cols) * 2 + side
        return pltpu.make_async_remote_copy(
            src_ref=slab(c, p, row), dst_ref=slab(c, p, row), send_sem=p_send.at[c, p, j],
            recv_sem=p_recv.at[c, p, j], device_id=(partner, at), device_id_type=MESH)

    def wanted(column):
        low = (2 * column * bulk + at) * tiles
        high = ((2 * column + 1) * bulk + at) * tiles + tiles - 1
        spots = [low, high] if slots == 2 else [low, low + tiles - 1, high]
        return [irrep_ref[s] for s in spots]

    def present(c):
        src = at + offsets[c]
        return jnp.logical_and(src >= 0, src < bulk)

    def relay(c, p):
        if offsets[c] <= 0:
            @pl.when(at < bulk - 1)
            def _():
                line(c, p, 1).start()
        if offsets[c] >= 0:
            @pl.when(at > 0)
            def _():
                line(c, p, -1).start()

    def relay_done(c, p):
        if offsets[c] <= 0 and offsets[c] - 1 > -bulk:
            @pl.when(at < bulk - 1)
            def _():
                line(c, p, 1).wait_send()
        if offsets[c] >= 0 and offsets[c] + 1 < bulk:
            @pl.when(at > 0)
            def _():
                line(c, p, -1).wait_send()

    def spread(c, p):
        src = amp if c == 0 else held[c][p]
        lanes = pl.ds(p * piece, piece) if c == 0 else slice(None)
        for j in range(1, cols):
            for s, g in enumerate(wanted(lax.rem(col + j, cols))):
                picked[c][p][j - 1, s] = src[g, lanes, :]
            across(c, p, j).start()
        first = pl.multiple_of((at + offsets[c]) * depth + p * piece, 16)
        for s, g in enumerate(wanted(col)):
            whole[s, pl.ds(first, piece), pl.ds(pl.multiple_of(me * width, 128), width)] = src[g, lanes, :]
        over(c, p, 0, core).start()

    def forward(c, p):
        for j in range(1, cols):
            across_in = pltpu.make_async_remote_copy(
                src_ref=slab(c, p, lax.rem(col - j + cols, cols) * 2 + core),
                dst_ref=slab(c, p, lax.rem(col - j + cols, cols) * 2 + core),
                send_sem=c_send.at[c, p, j], recv_sem=c_recv.at[c, p, j],
                device_id=(partner, at), device_id_type=MESH)
            across_in.wait_recv()
            over(c, p, j, core).start()

    for p in range(parts):
        relay(0, p)
    for p in range(parts):
        spread(0, p)
    groups = [[(0, p) for p in range(parts)]]
    for d in range(1, bulk):
        groups.append([(c, p) for p in range(parts) for c in (2 * d - 1, 2 * d)])
    for d in range(1, bulk):
        for c, p in groups[d]:
            @pl.when(present(c))
            def _():
                line_in(c, p).wait_recv()
                if abs(offsets[c]) < bulk - 1:
                    relay(c, p)
                spread(c, p)
        for c, p in groups[d - 1]:
            @pl.when(present(c))
            def _():
                forward(c, p)
    for c, p in groups[bulk - 1]:
        @pl.when(present(c))
        def _():
            forward(c, p)
    int_copy.wait()
    res_copy.wait()
    for group in groups:
        for c, p in group:
            @pl.when(present(c))
            def _():
                for j in range(cols):
                    over(c, p, j, 1 - core).wait_recv()

    mine = wanted(col)
    first_tile = (me * bulk + at) * tiles
    columns = whole.shape[2]
    block_n = 256 if columns % 256 == 0 else 128

    for t in range(tiles):
        irrep = irrep_ref[first_tile + t]
        slot = (irrep > mine[0]).astype(jnp.int32)
        for s in mine[1:-1]:
            slot = slot + (irrep > s).astype(jnp.int32)

        @pl.loop(0, columns // block_n)
        def _(n):
            span = pl.ds(pl.multiple_of(n * block_n, block_n), block_n)
            ladder = jnp.dot(ints[t], whole[slot, :, span], preferred_element_type=jnp.float32)
            out_ref[t, :, span] = (res[t, :, span].astype(jnp.float32) + ladder).astype(jnp.bfloat16)

    for group in groups:
        for c, p in group:
            @pl.when(present(c))
            def _():
                for j in range(cols):
                    over(c, p, j, core).wait_send()
                for j in range(1, cols):
                    across(c, p, j).wait_send()
                relay_done(c, p)

def call(rows, bulk, slots, integrals, amplitudes, residual_in, tile_irrep):
    irreps, depth, width = amplitudes.shape
    parts = PARTS if depth % (16 * PARTS) == 0 else 1
    chunks = 2 * bulk - 1
    cols = rows // 2
    any_space = pl.BlockSpec(memory_space=pl.ANY)
    return pl.pallas_call(
        functools.partial(kernel, rows, bulk, slots, parts),
        out_shape=jax.ShapeDtypeStruct(residual_in.shape, residual_in.dtype),
        in_specs=[pl.BlockSpec(memory_space=pltpu.SMEM), any_space, any_space, any_space],
        out_specs=pl.BlockSpec(memory_space=pltpu.VMEM),
        scratch_shapes=[
            pltpu.VMEM(amplitudes.shape, amplitudes.dtype),
            pltpu.VMEM(integrals.shape, integrals.dtype),
            pltpu.VMEM(residual_in.shape, residual_in.dtype),
            pltpu.VMEM((slots, depth * bulk, width * rows), amplitudes.dtype),
            *[pltpu.VMEM((irreps, depth // parts, width), amplitudes.dtype)] * ((chunks - 1) * parts),
            *[pltpu.VMEM((cols - 1, slots, depth // parts, width), amplitudes.dtype)] * (chunks * parts),
            pltpu.SemaphoreType.DMA((2, chunks, parts)),
            pltpu.SemaphoreType.DMA((chunks, parts)),
            pltpu.SemaphoreType.DMA((chunks, parts, cols)),
            pltpu.SemaphoreType.DMA((chunks, parts, cols)),
            pltpu.SemaphoreType.DMA((chunks, parts, cols)),
            pltpu.SemaphoreType.DMA((chunks, parts, cols)),
            pltpu.SemaphoreType.DMA((3,)),
        ],
        compiler_params=pltpu.CompilerParams(collective_id=slots, has_side_effects=True),
    )(tile_irrep, amplitudes, integrals, residual_in)


def local(rows, bulk, integrals, amplitudes, residual_in, tile_irrep):
    depth, width = amplitudes.shape[1:]
    if rows % 2 or rows < 4 or bulk < 2 or depth % 16 or width % 128:
        return gathered_plan(integrals, amplitudes, residual_in, tile_irrep)
    ends = tile_irrep.reshape(rows // 2, 2, bulk, integrals.shape[0])
    low, high = ends[:, 0, :, 0], ends[:, 1, :, -1]
    mid = ends[:, 0, :, -1]
    mid_too = ends[:, 1, :, 0]
    third = jnp.any(((mid != low) & (mid != high)) | ((mid_too != low) & (mid_too != high)))
    return lax.cond(
        third,
        functools.partial(call, rows, bulk, 3),
        functools.partial(call, rows, bulk, 2),
        integrals, amplitudes, residual_in, tile_irrep)


def solution(mesh):
    return jax.shard_map(
        functools.partial(local, mesh.shape["tile"], mesh.shape["bulk"]),
        mesh=mesh,
        in_specs=(
            P(("tile", "bulk"), None, None),
            P(None, "bulk", "tile"),
            P(("tile", "bulk"), None, None),
            P(),
        ),
        out_specs=P(("tile", "bulk"), None, None),
        check_vma=False,
    )
```

time: 96.1 us -> 33.8 us (0.35)
  waiting for transfers between devices: 47.6 us -> 0 us
  Pallas kernels: 0 us -> 30.3 us
  blocking collectives: 18.7 us -> 0 us
  between operations: 13.4 us -> 0.67 us
  local copies, waits for them, and re-layouts: 10.3 us -> 1.91 us
  matrix products: 5.4 us -> 0 us
    all_gather x1 -> x0, waiting for transfers between devices: 47.6 us -> none  [local(): lax.all_gather(whole_cd, 'tile', axis=2, tiled=True)]
    pallas_call x0 -> x1, Pallas kernels: none -> 30.3 us  [call(): pl.pallas_call(functools.partial(kernel, rows, bulk, slots, parts), out_s...]
    all_gather x1 -> x0, blocking collectives: 18.7 us -> none  [local(): whole_cd = lax.all_gather(amplitudes, 'bulk', axis=1, tiled=True)]
    gather x1 -> x0, local copies, waits for them, and re-layouts: 6.01 us -> none  [local(): jnp.take(lax.all_gather(whole_cd, 'tile', axis=2, tiled=True), local_irre...]
    dot_general x1 -> x0, matrix products: 5.4 us -> none  [local(): jnp.einsum('trc,tcp->trp', integrals, picked, preferred_element_type=jnp....]
    convert_element_type x1 -> x0, local copies, waits for them, and re-layouts: 2.58 us -> none  [local(): return (residual_in.astype(jnp.float32) + product).astype(jnp.bfloat16)]
  transfers between devices with their start and end apart: 1 -> 0, of which waited for: 1 -> 0; matrix products, arithmetic and copies ran while one was open for 2% -> 0% of each run, Pallas kernels for 0% -> 0%
where the time goes in v1:
time: 33.8 us; the launch traced here: 33.6 us
  Pallas kernels  30.3 us (90%)
  local copies, waits for them, and re-layouts  1.91 us (6%)
  other arithmetic  0.73 us (2%)
  between operations  0.67 us (2%)
    pallas_call x1, Pallas kernels, call(): pl.pallas_call(functools.partial(kernel, rows, bulk, slots, parts), out_s...  30.3 us
    unnamed x1, local copies, waits for them, and re-layouts  1.15 us
    reshape x1, local copies, waits for them, and re-layouts, local(): ends = tile_irrep.reshape(rows // 2, 2, bulk, integrals.shape[0])  0.76 us
    reduce_or x1, other arithmetic, local(): jnp.any((mid != low) & (mid != high) | (mid_too != low) & (mid_too != high))  0.73 us

profile of v1, /device:TPU:1, one launch (start us, length us, event | category | flops | bytes accessed | tf_op | source)
XLA Modules:
  0.0 33.6 jit_solution(13256715197945323760)
XLA Ops:
  0.0 0.8 %reshape.10 = s32[4,2,4,3]{3,2,1,0:T(4,128)S(1)} reshape(s32[96]{0:T(128)} %param.9) | data formatting | bytes 768 | tf_op jit(solution)/shard_map/reshape | solution.py:241
  0.8 0.7 %or_reduce_fusion = pred[]{:T(512)} fusion(s32[4,2,4,3]{3,2,1,0:T(4,128)S(1)} %reshape.10), kind=kLoop, calls=%fused_computation | loop fusion | flops 127 | bytes 257 | tf_op jit(solution)/shard_map/reduce_or | solution.py:245
  2.1 30.3 %conditional.1 = (bf16[3,256,1024]{2,1,0:T(8,128)(2,1)S(1)}) conditional(s32[]{:T(128)} %convert_element_type.3, (s32[96]{0:T(128)}, bf16[4,192,128]{2,1,0:T(8,128)(2,1)}, bf16[3,256,768]{2,1,0:T(8,128)(2,1)}, bf16[3,256,1024]{2,1,0:T(8,128)(2,1)}) %tuple.11, (s32[96]{0:T(128)}, bf16[4,192,128]{2,1,0:T(8,128)(2,1)}, bf16[3,256,768]{2,1,0:T(8,128)(2,1)}, ...), branch_computations={%region_1.0_spmd, %region_2.0_spmd} | conditional | bytes 8 | solution.py:246
  2.2 30.3 %branch_0_fun.1 = bf16[3,256,1024]{2,1,0:T(8,128)(2,1)S(1)} custom-call(s32[96]{0:T(128)} %get-tuple-element.24.irrep_ref, bf16[4,192,128]{2,1,0:T(8,128)(2,1)} %get-tuple-element.39.amp_hbm, bf16[3,256,768]{2,1,0:T(8,128)(2,1)} %get-tuple-element.41.int_hbm, bf16[3,256,1024]{2,1,0:T(8,128)(2,1)} %get-tuple-element.43.res_hbm), custom_call_target="tpu_custom_call" | custom-call | tf_op jit(solution)/shard_map/cond/branch_0_fun/pallas_call | solution.py:213
  32.5 1.1 %copy.16 = bf16[3,256,1024]{2,1,0:T(8,128)(2,1)} copy(bf16[3,256,1024]{2,1,0:T(8,128)(2,1)S(1)} %get-tuple-element.32) | data formatting | bytes 3145728

commit v2 on v1

--- a/solution.py
+++ b/solution.py
@@ -180,7 +180,7 @@
     mine = wanted(col)
     first_tile = (me * bulk + at) * tiles
     columns = whole.shape[2]
-    block_n = 256 if columns % 256 == 0 else 128
+    block_n = 512 if columns % 512 == 0 else 128
 
     for t in range(tiles):
         irrep = irrep_ref[first_tile + t]

time: 33.8 us -> 32.6 us (0.964)
  Pallas kernels: 30.3 us -> 29.1 us
    pallas_call x1, Pallas kernels: 30.3 us -> 29.1 us  [call(): pl.pallas_call(functools.partial(kernel, rows, bulk, slots, parts), out_s...]
where the time goes in v2:
time: 32.6 us; the launch traced here: 32.4 us
  Pallas kernels  29.1 us (89%)
  local copies, waits for them, and re-layouts  1.91 us (6%)
  other arithmetic  0.73 us (2%)
  between operations  0.67 us (2%)
    pallas_call x1, Pallas kernels, call(): pl.pallas_call(functools.partial(kernel, rows, bulk, slots, parts), out_s...  29.1 us
    unnamed x1, local copies, waits for them, and re-layouts  1.15 us
    reshape x1, local copies, waits for them, and re-layouts, local(): ends = tile_irrep.reshape(rows // 2, 2, bulk, integrals.shape[0])  0.76 us
    reduce_or x1, other arithmetic, local(): jnp.any((mid != low) & (mid != high) | (mid_too != low) & (mid_too != high))  0.73 us

profile of v2, /device:TPU:1, one launch (start us, length us, event | category | flops | bytes accessed | tf_op | source)
XLA Modules:
  0.0 32.4 jit_solution(9227728659625788692)
XLA Ops:
  0.0 0.8 %reshape.10 = s32[4,2,4,3]{3,2,1,0:T(4,128)S(1)} reshape(s32[96]{0:T(128)} %param.9) | data formatting | bytes 768 | tf_op jit(solution)/shard_map/reshape | solution.py:241
  0.8 0.7 %or_reduce_fusion = pred[]{:T(512)} fusion(s32[4,2,4,3]{3,2,1,0:T(4,128)S(1)} %reshape.10), kind=kLoop, calls=%fused_computation | loop fusion | flops 127 | bytes 257 | tf_op jit(solution)/shard_map/reduce_or | solution.py:245
  2.1 29.2 %conditional.1 = (bf16[3,256,1024]{2,1,0:T(8,128)(2,1)S(1)}) conditional(s32[]{:T(128)} %convert_element_type.3, (s32[96]{0:T(128)}, bf16[4,192,128]{2,1,0:T(8,128)(2,1)}, bf16[3,256,768]{2,1,0:T(8,128)(2,1)}, bf16[3,256,1024]{2,1,0:T(8,128)(2,1)}) %tuple.11, (s32[96]{0:T(128)}, bf16[4,192,128]{2,1,0:T(8,128)(2,1)}, bf16[3,256,768]{2,1,0:T(8,128)(2,1)}, ...), branch_computations={%region_1.0_spmd, %region_2.0_spmd} | conditional | bytes 8 | solution.py:246
  2.2 29.1 %branch_0_fun.1 = bf16[3,256,1024]{2,1,0:T(8,128)(2,1)S(1)} custom-call(s32[96]{0:T(128)} %get-tuple-element.24.irrep_ref, bf16[4,192,128]{2,1,0:T(8,128)(2,1)} %get-tuple-element.39.amp_hbm, bf16[3,256,768]{2,1,0:T(8,128)(2,1)} %get-tuple-element.41.int_hbm, bf16[3,256,1024]{2,1,0:T(8,128)(2,1)} %get-tuple-element.43.res_hbm), custom_call_target="tpu_custom_call" | custom-call | tf_op jit(solution)/shard_map/cond/branch_0_fun/pallas_call | solution.py:213
  31.3 1.1 %copy.16 = bf16[3,256,1024]{2,1,0:T(8,128)(2,1)} copy(bf16[3,256,1024]{2,1,0:T(8,128)(2,1)S(1)} %get-tuple-element.32) | data formatting | bytes 3145728
